TPU v7x, 32 devices: a whole 2x2x4 slice. The times are simulated.
32 devices in a mesh: gx: 2 (over x), gy: 4 (over y, core), gz: 4 (over z).
Axes of the slice: x: 2, y: 2, z: 4, core: 2. Of those that a mesh axis runs over, the one named last changes fastest.
Arguments:
- query: bfloat16 [4, 4, 4096], replicated, may hold values from -50 to 50
- keys: bfloat16 [4096, 4, 4096], P(('gx', 'gy', 'gz')), may hold values from -6 to 6
- values: bfloat16 [4096, 4, 4096], P(('gx', 'gy', 'gz')), may hold values from -6 to 6
- lm_keys: bfloat16 [128, 4, 4096], P(('gx', 'gy', 'gz')), may hold values from -10 to 10
- lm_values: bfloat16 [128, 4, 4096], P(('gx', 'gy', 'gz')), may hold values from -6 to 6
- selected: int32 [4, 16, 16], replicated, may hold values from 0 to 127, as said below
Outputs:
- attended: float32 [4, 4, 4096], P(None, None, ('gx', 'gy', 'gz'))
Inputs may be any that keep to these rules, and one draw needn't show every extreme that they name: `selected`: each batch row and head names 16 different blocks; every shard holds either none of them or exactly 2.
All inputs are finite; a program needn't handle non-finite values.
Results may differ from a plain program's by a relative error of at most 0.0007.
Values sent between devices are 32-bit elements; how exact they have to be, the bound alone decides.
A program may use at most 64 MiB of HBM per device.

v0:
```python
import math
import jax
import jax.numpy as jnp
from jax import lax
from jax.sharding import PartitionSpec as P


def body(query, keys, values, lm_keys, lm_values, selected):
    device_count = lax.axis_size(("gx", "gy", "gz"))
    my_index = lax.axis_index(("gx", "gy", "gz"))
    positions, batch_rows, feature_width = keys.shape
    local_blocks = lm_keys.shape[0]
    block_len = positions // local_blocks
    head_count = selected.shape[1]
    head_width = feature_width // head_count
    draft_count = query.shape[1]
    query_heads = query.reshape(batch_rows, draft_count, head_count, head_width)
    score_scale = 1.0 / math.sqrt(head_width)
    block_ids = my_index * local_blocks + jnp.arange(local_blocks, dtype=jnp.int32)
    chosen_here = jnp.any(selected[:, :, :, None] == block_ids[None, None, None, :], axis=2)
    summary_keys = lm_keys.reshape(local_blocks, batch_rows, head_count, head_width)
    summary_values = lm_values.reshape(local_blocks, batch_rows, head_count, head_width)
    summary_score = (
        jnp.einsum("bphd,lbhd->bphl", query_heads, summary_keys, preferred_element_type=jnp.float32)
        * score_scale
    )
    keys_heads = keys.reshape(positions, batch_rows, head_count, head_width)
    values_heads = values.reshape(positions, batch_rows, head_count, head_width)
    live_tokens = jnp.repeat(chosen_here, block_len, axis=2)
    token_score = (
        jnp.einsum("bphd,tbhd->bpht", query_heads, keys_heads, preferred_element_type=jnp.float32)
        * score_scale
    )
    token_score = jnp.where(live_tokens[:, None], token_score, -jnp.inf)
    local_peak = jnp.maximum(jnp.max(token_score, -1), jnp.max(summary_score, -1))
    token_weight = jnp.exp(token_score - local_peak[..., None])
    summary_weight = jnp.exp(summary_score - local_peak[..., None])
    local_total = jnp.sum(token_weight, -1) + jnp.sum(summary_weight, -1)
    local_sum = jnp.einsum(
        "bpht,tbhd->bphd",
        token_weight.astype(jnp.bfloat16),
        values_heads,
        preferred_element_type=jnp.float32,
    ) + jnp.einsum(
        "bphl,lbhd->bphd",
        summary_weight.astype(jnp.bfloat16),
        summary_values,
        preferred_element_type=jnp.float32,
    )
    column_count = feature_width // device_count
    global_peak = lax.pmax(local_peak, ("gx", "gy", "gz"))
    rescale = jnp.exp(local_peak - global_peak)
    denominator, numerator = lax.psum(
        (local_total * rescale, local_sum * rescale[..., None]), ("gx", "gy", "gz")
    )
    own_numerator = lax.dynamic_slice_in_dim(
        numerator.reshape(batch_rows, draft_count, feature_width),
        my_index * column_count,
        column_count,
        2,
    )
    spread_denominator = jnp.repeat(denominator, head_width, axis=2)
    own_denominator = lax.dynamic_slice_in_dim(
        spread_denominator, my_index * column_count, column_count, 2
    )
    return own_numerator / own_denominator


def solution(mesh):
    placed = (
        P(),
        P(("gx", "gy", "gz"), None, None),
        P(("gx", "gy", "gz"), None, None),
        P(("gx", "gy", "gz"), None, None),
        P(("gx", "gy", "gz"), None, None),
        P(),
    )
    return jax.shard_map(
        body,
        mesh=mesh,
        in_specs=placed,
        out_specs=P(None, None, ("gx", "gy", "gz")),
        check_vma=False,
    )
```

profile of v0, /device:TPU:0, one launch (start us, length us, event | category | flops | bytes accessed | tf_op | source)
XLA Modules:
  0.0 211.6 jit_solution(752959228649032096)
XLA Ops:
  6.5 0.0 copy-start
  6.5 0.0 all-reduce.2.cloned.1.call-start
  6.5 1.2 compare_reduce_fusion
  7.8 0.1 copy.15
  7.9 0.1 broadcast_in_dim.25
  8.0 0.1 broadcast_in_dim.26
  8.1 0.0 copy-start.1
  8.2 7.7 %reshape.33 = bf16[128,4,16,256]{3,2,1,0:T(8,128)(2,1)} reshape(bf16[128,4,4096]{2,1,0:T(4,128)(2,1)} %param.7) | data formatting | bytes 8388608 | tf_op jit(solution)/shard_map/reshape | solution.py:27
  15.9 0.0 copy-done.1
  15.9 0.1 reshape.35
  16.0 0.0 copy-done
  16.0 0.2 fusion.27
  16.2 4.6 %fusion.26 = (f32[4,4,16]{1,2,0:T(8,128)S(1)}, f32[4,4,16,128]{3,1,2,0:T(4,128)S(1)}) fusion(bf16[4,4,16,256]{3,1,2,0:T(4,128)(2,1)S(1)} %bitcast.15, bf16[128,4,16,256]{3,2,1,0:T(8,128)(2,1)} %reshape.33, pred[4,16,128]{2,1,0:T(8,128)(4,1)S(1)} %broadcast_in_dim.26), kind=kOutput, calls=%fused_computation.27 | convolution fusion | flops 16875264 | bytes 4465664 | tf_op jit(solution)/shard_map/bphd,tbhd->bpht/dot_general | solution.py:31
  20.9 42.1 %pmax.7 = f32[4,4,16]{1,2,0:T(8,128)S(1)} all-reduce(f32[4,4,16]{1,2,0:T(8,128)S(1)} %max.9), channel_id=1, replica_groups=mesh['gx'=2,'gy'=4,'gz'=4] {'gx','gy','gz'}, use_global_device_ids=true, to_apply=%region_3.4 | all-reduce | flops 256 | bytes 2048 | tf_op jit(solution)/shard_map/pmax | solution.py:51
  63.0 0.3 fusion.18
  63.2 0.1 fusion.20
  63.4 7.7 %reshape.36 = bf16[128,4,16,256]{3,2,1,0:T(8,128)(2,1)} reshape(bf16[128,4,4096]{2,1,0:T(4,128)(2,1)} %param.8) | data formatting | bytes 8388608 | tf_op jit(solution)/shard_map/reshape | solution.py:28
  71.1 0.0 copy-start.2
  71.1 4.6 %fusion = f32[4,16,4,256]{3,2,1,0:T(4,128)S(1)} fusion(bf16[128,4,16,256]{3,2,1,0:T(8,128)(2,1)} %reshape.36, f32[4,4,16,128]{3,1,2,0:T(4,128)S(1)} %get-tuple-element.8, f32[4,4,16]{1,2,0:T(8,128)S(1)} %max.9), kind=kOutput, calls=%fused_computation | convolution fusion | flops 16842752 | bytes 4588544 | tf_op jit(solution)/shard_map/bpht,tbhd->bphd/dot_general | solution.py:39
  75.7 0.0 copy-done.2
  75.7 0.1 reshape.37
  75.8 1.0 fusion.5
  76.7 0.0 all-reduce.2.cloned.1.call-update
  76.8 40.3 %psum.15 = f32[4,4,16]{1,2,0:T(8,128)S(1)} all-reduce(f32[4,4,16]{1,2,0:T(8,128)S(1)} %get-tuple-element.5), channel_id=1, replica_groups=mesh['gx'=2,'gy'=4,'gz'=4] {'gx','gy','gz'}, use_global_device_ids=true, to_apply=%region_7.8 | all-reduce | flops 256 | bytes 2048 | tf_op jit(solution)/shard_map/psum | solution.py:53
  117.1 0.1 copy.23
  117.2 0.1 broadcast_in_dim.29
  117.3 0.1 reshape.39
  117.4 86.0 %all-reduce.2.cloned.1.call-done = f32[4,4,4096]{2,1,0:T(4,128)} async-done(((f32[4,4,4096]{2,1,0:T(4,128)}), f32[4,4,4096]{2,1,0:T(4,128)}) %all-reduce.2.cloned.1.call-update) | async-done | bytes 262160 | tf_op jit(solution)/shard_map/psum | solution.py:53
  203.4 1.3 dynamic-slice_divide_fusion
  (3 shorter events, 0.0 us)
Async XLA Ops:
  6.5 9.4 %copy-start = (bf16[4,4,4096]{2,1,0:T(4,128)(2,1)S(1)}, bf16[4,4,4096]{2,1,0:T(4,128)(2,1)}, u32[]{:S(2)}) copy-start(bf16[4,4,4096]{2,1,0:T(4,128)(2,1)} %param.6) | copy-start | bytes 393220
  6.5 196.9 %all-reduce.2.cloned.1.call-start = ((), (), s32[]{:S(2)}) async-start(), calls=%async_computation | async-start | bytes 524288 | tf_op jit(solution)/shard_map/psum | solution.py:53
  8.1 7.8 %copy-start.1 = (bf16[4,4,4096]{2,1,0:T(4,128)(2,1)S(1)}, bf16[4,4,4096]{2,1,0:T(4,128)(2,1)}, u32[]{:S(2)}) copy-start(bf16[4,4,4096]{2,1,0:T(4,128)(2,1)} %param.9) | copy-start | bytes 393220
  71.1 4.6 %copy-start.2 = (bf16[4,4,4096]{2,1,0:T(4,128)(2,1)S(1)}, bf16[4,4,4096]{2,1,0:T(4,128)(2,1)}, u32[]{:S(2)}) copy-start(bf16[4,4,4096]{2,1,0:T(4,128)(2,1)} %param.10) | copy-start | bytes 393220
Sparse Core Ops, SparseCore 0:
  76.9 126.4 all-reduce.1
where the time goes:
time: 212 us
  waiting for transfers between devices  86 us (41%)
  blocking collectives  82.4 us (39%)
  local copies, waits for them, and re-layouts  16.3 us (8%)
  between operations  13.5 us (6%)
  matrix products  10.4 us (5%)
  other arithmetic  2.92 us (1%)
    psum x1, waiting for transfers between devices, body(): lax.psum((local_total * rescale, local_sum * rescale[..., None]), ('gx',...  86 us
    pmax x1, blocking collectives, body(): global_peak = lax.pmax(local_peak, ('gx', 'gy', 'gz'))  42.1 us
    psum x1, blocking collectives, body(): lax.psum((local_total * rescale, local_sum * rescale[..., None]), ('gx',...  40.3 us
    reshape x1, local copies, waits for them, and re-layouts, body(): keys_heads = keys.reshape(positions, batch_rows, head_count, head_width)  7.75 us
    reshape x1, local copies, waits for them, and re-layouts, body(): values_heads = values.reshape(positions, batch_rows, head_count, head_width)  7.71 us
    dot_general x1, matrix products, body(): jnp.einsum('bphd,tbhd->bpht', query_heads, keys_heads, preferred_element_...  4.65 us
    dot_general x1, matrix products, body(): jnp.einsum('bpht,tbhd->bphd', token_weight.astype(jnp.bfloat16), values_h...  4.58 us
  transfers between devices with their start and end apart: 1, of which 1 were waited for; matrix products, arithmetic and copies ran while one was open for 0% of the time, Pallas kernels for 0%

commit v1 on v0

--- a/solution.py
+++ b/solution.py
@@ -51,7 +51,7 @@
     global_peak = lax.pmax(local_peak, ("gx", "gy", "gz"))
     rescale = jnp.exp(local_peak - global_peak)
     denominator, numerator = lax.psum(
-        (local_total * rescale, local_sum * rescale[..., None]), ("gx", "gy", "gz")
+        lax.psum((local_total * rescale, local_sum * rescale[..., None]), ("gy", "gz")), "gx"
     )
     own_numerator = lax.dynamic_slice_in_dim(
         numerator.reshape(batch_rows, draft_count, feature_width),

time: 212 us -> 245 us (1.16)
  blocking collectives: 82.4 us -> 111 us
  waiting for transfers between devices: 86 us -> 89.8 us
    psum x1 -> x2, blocking collectives: 40.3 us -> 69 us  [the longest x1 60.7 us: body(): lax.psum((local_total * rescale, local_sum * rescale[..., None]), ('gy',...]
    psum x1 -> x2, waiting for transfers between devices: 86 us -> 89.8 us  [the longest x1 89.7 us: body(): lax.psum((local_total * rescale, local_sum * rescale[..., None]), ('gy',...]
  transfers between devices with their start and end apart: 1 -> 2, of which waited for: 1 -> 1; matrix products, arithmetic and copies ran while one was open for 0% -> 0% of each run, Pallas kernels for 0% -> 0%
where the time goes in v1:
time: 245 us; the launch traced here: 244 us
  blocking collectives  111 us (45%)
  waiting for transfers between devices  89.8 us (37%)
  local copies, waits for them, and re-layouts  16.3 us (7%)
  between operations  13.5 us (6%)
  matrix products  10.4 us (4%)
  other arithmetic  2.93 us (1%)
    psum x1, waiting for transfers between devices, body(): lax.psum((local_total * rescale, local_sum * rescale[..., None]), ('gy',...  89.7 us
    psum x1, blocking collectives, body(): lax.psum((local_total * rescale, local_sum * rescale[..., None]), ('gy',...  60.7 us
    pmax x1, blocking collectives, body(): global_peak = lax.pmax(local_peak, ('gx', 'gy', 'gz'))  42.1 us
    psum x1, blocking collectives, body(): lax.psum(lax.psum((local_total * rescale, local_sum * rescale[..., None])...  8.3 us
    reshape x1, local copies, waits for them, and re-layouts, body(): keys_heads = keys.reshape(positions, batch_rows, head_count, head_width)  7.75 us
    reshape x1, local copies, waits for them, and re-layouts, body(): values_heads = values.reshape(positions, batch_rows, head_count, head_width)  7.71 us
  transfers between devices with their start and end apart: 2, of which 1 were waited for; matrix products, arithmetic and copies ran while one was open for 0% of the time, Pallas kernels for 0%

profile of v1, /device:TPU:0, one launch (start us, length us, event | category | flops | bytes accessed | tf_op | source)
XLA Modules:
  0.0 244.1 jit_solution(7350634668371081787)
XLA Ops:
  6.5 0.0 copy-start
  6.5 0.0 all-reduce.3.cloned.1.call-start
  6.5 1.2 compare_reduce_fusion
  7.8 0.1 copy.15
  7.9 0.1 broadcast_in_dim.25
  8.0 0.1 broadcast_in_dim.26
  8.1 0.0 copy-start.1
  8.2 7.7 %reshape.33 = bf16[128,4,16,256]{3,2,1,0:T(8,128)(2,1)} reshape(bf16[128,4,4096]{2,1,0:T(4,128)(2,1)} %param.7) | data formatting | bytes 8388608 | tf_op jit(solution)/shard_map/reshape | solution.py:27
  15.9 0.0 copy-done.1
  15.9 0.1 reshape.35
  16.0 0.0 copy-done
  16.0 0.2 fusion.27
  16.2 4.6 %fusion.26 = (f32[4,4,16]{1,2,0:T(8,128)S(1)}, f32[4,4,16,128]{3,1,2,0:T(4,128)S(1)}) fusion(bf16[4,4,16,256]{3,1,2,0:T(4,128)(2,1)S(1)} %bitcast.15, bf16[128,4,16,256]{3,2,1,0:T(8,128)(2,1)} %reshape.33, pred[4,16,128]{2,1,0:T(8,128)(4,1)S(1)} %broadcast_in_dim.26), kind=kOutput, calls=%fused_computation.27 | convolution fusion | flops 16875264 | bytes 4465664 | tf_op jit(solution)/shard_map/bphd,tbhd->bpht/dot_general | solution.py:31
  20.9 42.1 %pmax.7 = f32[4,4,16]{1,2,0:T(8,128)S(1)} all-reduce(f32[4,4,16]{1,2,0:T(8,128)S(1)} %max.9), channel_id=1, replica_groups=mesh['gx'=2,'gy'=4,'gz'=4] {'gx','gy','gz'}, use_global_device_ids=true, to_apply=%region_3.4 | all-reduce | flops 256 | bytes 2048 | tf_op jit(solution)/shard_map/pmax | solution.py:51
  63.0 0.3 fusion.18
  63.2 0.1 fusion.20
  63.4 7.7 %reshape.36 = bf16[128,4,16,256]{3,2,1,0:T(8,128)(2,1)} reshape(bf16[128,4,4096]{2,1,0:T(4,128)(2,1)} %param.8) | data formatting | bytes 8388608 | tf_op jit(solution)/shard_map/reshape | solution.py:28
  71.1 0.0 copy-start.2
  71.1 4.6 %fusion = f32[4,16,4,256]{3,2,1,0:T(4,128)S(1)} fusion(bf16[128,4,16,256]{3,2,1,0:T(8,128)(2,1)} %reshape.36, f32[4,4,16,128]{3,1,2,0:T(4,128)S(1)} %get-tuple-element.8, f32[4,4,16]{1,2,0:T(8,128)S(1)} %max.9), kind=kOutput, calls=%fused_computation | convolution fusion | flops 16842752 | bytes 4588544 | tf_op jit(solution)/shard_map/bpht,tbhd->bphd/dot_general | solution.py:39
  75.6 0.0 copy-done.2
  75.6 0.1 reshape.37
  75.8 1.0 fusion.5
  76.7 0.0 all-reduce.3.cloned.1.call-update
  76.8 0.0 all-reduce.5.cloned.1.call-start
  76.8 89.7 %all-reduce.3.cloned.1.call-done = f32[4,4,16,256]{3,1,2,0:T(4,128)} async-done(((f32[4,4,16,256]{3,1,2,0:T(4,128)}), f32[4,4,16,256]{3,1,2,0:T(4,128)}) %all-reduce.3.cloned.1.call-update) | async-done | bytes 262160 | tf_op jit(solution)/shard_map/psum | solution.py:54
  166.6 0.0 all-reduce.5.cloned.1.call-update
  166.6 60.7 %psum.30 = f32[4,4,16]{1,2,0:T(8,128)S(1)} all-reduce(f32[4,4,16]{1,2,0:T(8,128)S(1)} %get-tuple-element.5), channel_id=1, replica_groups=mesh['gx'=2,'gy'=4,'gz'=4] {'gy','gz'}, use_global_device_ids=true, to_apply=%region_8.9 | all-reduce | flops 256 | bytes 2048 | tf_op jit(solution)/shard_map/psum | solution.py:54
  227.3 8.3 %psum.31 = f32[4,4,16]{1,2,0:T(8,128)S(1)} all-reduce(f32[4,4,16]{1,2,0:T(8,128)S(1)} %psum.30), channel_id=1, replica_groups=mesh['gx'=2,'gy'=4,'gz'=4] {'gx'}, use_global_device_ids=true, to_apply=%region_9.10 | all-reduce | flops 256 | bytes 2048 | tf_op jit(solution)/shard_map/psum | solution.py:53
  235.6 0.1 copy.23
  235.7 0.1 broadcast_in_dim.29
  235.8 0.1 reshape.39
  235.9 0.0 all-reduce.5.cloned.1.call-done
  235.9 1.3 dynamic-slice_divide_fusion
  (3 shorter events, 0.0 us)
Async XLA Ops:
  6.5 9.4 %copy-start = (bf16[4,4,4096]{2,1,0:T(4,128)(2,1)S(1)}, bf16[4,4,4096]{2,1,0:T(4,128)(2,1)}, u32[]{:S(2)}) copy-start(bf16[4,4,4096]{2,1,0:T(4,128)(2,1)} %param.6) | copy-start | bytes 393220
  6.5 160.0 %all-reduce.3.cloned.1.call-start = ((), (), s32[]{:S(2)}) async-start(), calls=%async_computation | async-start | bytes 524288 | tf_op jit(solution)/shard_map/psum | solution.py:54
  8.1 7.8 %copy-start.1 = (bf16[4,4,4096]{2,1,0:T(4,128)(2,1)S(1)}, bf16[4,4,4096]{2,1,0:T(4,128)(2,1)}, u32[]{:S(2)}) copy-start(bf16[4,4,4096]{2,1,0:T(4,128)(2,1)} %param.9) | copy-start | bytes 393220
  71.1 4.6 %copy-start.2 = (bf16[4,4,4096]{2,1,0:T(4,128)(2,1)S(1)}, bf16[4,4,4096]{2,1,0:T(4,128)(2,1)}, u32[]{:S(2)}) copy-start(bf16[4,4,4096]{2,1,0:T(4,128)(2,1)} %param.10) | copy-start | bytes 393220
  76.8 159.2 %all-reduce.5.cloned.1.call-start = ((), (), s32[]{:S(2)}) async-start(), calls=%async_computation.1 | async-start | bytes 524288 | tf_op jit(solution)/shard_map/psum | solution.py:53
Sparse Core Ops, SparseCore 0:
  76.9 89.6 all-reduce.2
  168.8 23.7 all-reduce.4
